TPU v7x, 128 devices: a whole 4x4x4 slice. The times are simulated.
128 devices in a mesh: gx: 4 (over z_hi, core), gy: 4 (over y), gz: 8 (over z_lo, x).
Axes of the slice: x: 4, y: 4, z: 4 (z_hi: 2, z_lo: 2; z = z_hi * 2 + z_lo), core: 2. Of those that a mesh axis runs over, the one named last changes fastest.
Arguments:
- grads: bfloat16 [8, 2048, 3584], P('gz', ('gx', 'gy')), may hold values from -300 to 300
- momentum: float32 [2048, 3584], P(('gx', 'gy')), may hold values from -0.8 to 0.8
- variance: float32 [2048, 3584], P(('gx', 'gy'), 'gz'), may hold values from 0.25 to 4
- master: float32 [2048, 3584], P(('gx', 'gy', 'gz')), may hold values from -6 to 6
Outputs:
- weights: bfloat16 [2048, 3584], replicated
- new_master: float32 [2048, 3584], P(('gx', 'gy', 'gz'))
- new_momentum: float32 [2048, 3584], P(('gx', 'gy', 'gz'))
- worker_error: float32 [8, 2048, 3584], P('gz', ('gx', 'gy'))
All inputs are finite; a program needn't handle non-finite values.
Results may differ from a plain program's by a relative error of at most 0.007.
Values may be sent and summed in bfloat16 or wider, within the bound.
A program may use at most 128 MiB of HBM per device.

v0:
```python
import jax
import jax.numpy as jnp
from jax import lax
from jax.sharding import PartitionSpec as P

beta_one = 0.9
learning_rate = 0.25
epsilon = 1e-08


def from_everyone(x, axis):
    copies = jnp.broadcast_to(x, (lax.axis_size(axis), *x.shape))
    return lax.all_to_all(copies, axis, split_axis=0, concat_axis=0, tiled=True)


def joined_along(blocks, dim):
    blocks = jnp.moveaxis(blocks, 0, dim)
    shape = blocks.shape
    return blocks.reshape(*shape[:dim], shape[dim] * shape[dim + 1], *shape[dim + 2 :])


def collect(x, axis, dim):
    blocks = from_everyone(x, axis)
    return joined_along(blocks, dim)


def shards(grads, momentum, variance, master):
    owned_variance = lax.all_to_all(
        variance.astype(jnp.bfloat16), "gz", split_axis=0, concat_axis=1, tiled=True
    ).astype(variance.dtype)
    corrected = beta_one * momentum + (1.0 - beta_one) * grads[0].astype(jnp.float32)
    level = jnp.mean(jnp.abs(corrected), axis=-1, keepdims=True).astype(jnp.bfloat16)
    signs = jnp.where(corrected >= 0.0, 1.0, -1.0).astype(jnp.float32)
    compressed = (level.astype(jnp.float32) * signs).astype(jnp.bfloat16)
    worker_error = (corrected - compressed.astype(jnp.float32))[None]
    received = lax.all_to_all(compressed[:, None, :], "gz", split_axis=0, concat_axis=1, tiled=True)
    new_momentum = jnp.sum(received.astype(jnp.float32), axis=1) / received.shape[1]
    new_master = master - learning_rate * new_momentum / (jnp.sqrt(owned_variance) + epsilon)
    shard = new_master.astype(jnp.bfloat16)
    gathered = collect(shard, "gz", 0)
    weights = lax.all_gather(gathered, ("gx", "gy"), axis=0, tiled=True)
    return (weights, new_master, new_momentum, worker_error)


def solution(mesh):
    return jax.shard_map(
        shards,
        mesh=mesh,
        in_specs=(
            P("gz", ("gx", "gy"), None),
            P(("gx", "gy"), None),
            P(("gx", "gy"), "gz"),
            P(("gx", "gy", "gz"), None),
        ),
        out_specs=(
            P(),
            P(("gx", "gy", "gz"), None),
            P(("gx", "gy", "gz"), None),
            P("gz", ("gx", "gy"), None),
        ),
        check_vma=False,
    )
```

profile of v0, /device:TPU:1, one launch (start us, length us, event | category | flops | bytes accessed | tf_op | source)
XLA Modules:
  0.0 189.1 jit_solution(6112298998503527955)
XLA Ops:
  7.2 0.0 copy-start
  7.2 0.0 copy-start.1
  7.2 1.8 copy.15
  9.0 6.2 %all-to-all-start.1 = ((bf16[8,16,448]{2,1,0:T(8,128)(2,1)}), bf16[8,16,448]{2,1,0:T(8,128)(2,1)S(1)}, u32[]{:S(2)}, u32[]{:S(2)}) async-start(bf16[8,16,448]{2,1,0:T(8,128)(2,1)} %bitcast.2), calls=%async_computation.1 | async-start | bytes 262144 | tf_op jit(solution)/shard_map/all_to_all | solution.py:28
  15.2 2.2 %abs_reduce_fusion = f32[128]{0:T(128)S(1)} fusion(bf16[1,128,3584]{2,1,0:T(8,128)(2,1)} %param.4, f32[128,3584]{1,0:T(8,128)} %param.5), kind=kLoop, calls=%fused_computation.3 | loop fusion | flops 2752384 | bytes 2753024 | tf_op jit(solution)/shard_map/reduce_sum | solution.py:32
  17.5 0.0 copy-done
  17.5 0.0 copy-done.1
  17.5 2.1 %subtract_bitcast_fusion = (f32[1,128,3584]{2,1,0:T(8,128)}, bf16[128,1,3584]{2,0,1:T(8,128)(2,1)}) fusion(f32[128]{0:T(128)S(1)} %convert_convert_fusion, bf16[1,128,3584]{2,1,0:T(8,128)(2,1)S(1)} %copy-done.1, f32[128,3584]{1,0:T(8,128)S(1)} %copy-done), kind=kLoop, calls=%fused_computation.1 | loop fusion | flops 4587520 | bytes 5505536 | tf_op jit(solution)/shard_map/broadcast_in_dim | solution.py:35
  19.5 0.5 broadcast.14
  20.0 2.5 %reduce.3 = bf16[128,3584]{1,0:T(8,128)(2,1)S(1)} reduce(bf16[128,1,3584]{2,0,1:T(8,128)(2,1)} %get-tuple-element.7, bf16[]{:T(256)} %broadcast.14), dimensions={1}, to_apply=%copy.14.reduce_sub_computation | reduce | bytes 1835010 | tf_op jit(solution)/shard_map/broadcast_in_dim | solution.py:36
  22.5 1.6 reshape.35
  24.1 0.0 all-to-all-done.1
  24.1 5.1 %all-to-all-start = ((bf16[8,2,28672]{2,1,0:T(2,128)(2,1)}), bf16[8,2,28672]{2,1,0:T(2,128)(2,1)S(1)}, u32[]{:S(2)}, u32[]{:S(2)}) async-start(bf16[8,2,28672]{2,1,0:T(2,128)(2,1)} %reshape.35), calls=%async_computation | async-start | bytes 1835008 | tf_op jit(solution)/shard_map/all_to_all | solution.py:36
  29.3 0.0 all-gather.2.cloned.1.call-start
  29.3 0.1 add_bitcast_fusion
  29.4 0.2 copy.16
  29.6 0.1 add.19
  29.7 14.0 %all-to-all-done = bf16[8,2,28672]{2,1,0:T(2,128)(2,1)S(1)} async-done(((bf16[8,2,28672]{2,1,0:T(2,128)(2,1)}), bf16[8,2,28672]{2,1,0:T(2,128)(2,1)S(1)}, u32[]{:S(2)}, u32[]{:S(2)}) %all-to-all-start) | async-done | bytes 917536 | tf_op jit(solution)/shard_map/all_to_all | solution.py:36
  43.7 3.3 %reshape.36 = bf16[128,1,3584]{2,1,0:T(2,128)(2,1)} reshape(bf16[8,2,28672]{2,1,0:T(2,128)(2,1)S(1)} %all-to-all-done) | data formatting | bytes 1835008
  47.0 1.6 copy.17
  48.6 0.0 copy-start.2
  48.7 0.1 reduce_sum.19
  48.8 0.8 copy-done.2
  49.6 0.8 fusion.1
  50.4 0.1 broadcast_in_dim.21
  50.5 17.1 %all_to_all.27 = bf16[8,16,3584]{2,1,0:T(8,128)(2,1)} all-to-all(bf16[8,16,3584]{2,1,0:T(8,128)(2,1)S(1)} %broadcast_in_dim.21), channel_id=1, replica_groups=mesh['gx'=4,'gy'=4,'gz'=8] {'gz'}, dimensions={0} | all-to-all | bytes 1835008 | tf_op jit(solution)/shard_map/all_to_all | solution.py:13
  67.5 0.0 all-gather.2.cloned.1.call-update
  67.6 101.6 %all-gather.2.cloned.1.call-done = bf16[2048,3584]{1,0:T(8,128)(2,1)} async-done(((bf16[128,3584]{1,0:T(8,128)(2,1)}), bf16[2048,3584]{1,0:T(8,128)(2,1)}) %all-gather.2.cloned.1.call-update) | async-done | bytes 14680080 | tf_op jit(solution)/shard_map/all_gather | solution.py:41
  169.2 13.1 %copy.20 = bf16[2048,3584]{1,0:T(8,128)(2,1)} copy(bf16[2048,3584]{1,0:T(8,128)(2,1)} %all-gather.2.cloned.1.call-done) | data formatting | bytes 29360128
  (1 shorter events, 0.0 us)
Async XLA Ops:
  7.2 10.3 %copy-start = (f32[128,3584]{1,0:T(8,128)S(1)}, f32[128,3584]{1,0:T(8,128)}, u32[]{:S(2)}) copy-start(f32[128,3584]{1,0:T(8,128)} %param.5) | copy-start | bytes 5505028
  7.2 10.3 %copy-start.1 = (bf16[1,128,3584]{2,1,0:T(8,128)(2,1)S(1)}, bf16[1,128,3584]{2,1,0:T(8,128)(2,1)}, u32[]{:S(2)}) copy-start(bf16[1,128,3584]{2,1,0:T(8,128)(2,1)} %param.4) | copy-start | bytes 2752516
  9.0 15.1 %all-to-all-start.1 = ((bf16[8,16,448]{2,1,0:T(8,128)(2,1)}), bf16[8,16,448]{2,1,0:T(8,128)(2,1)S(1)}, u32[]{:S(2)}, u32[]{:S(2)}) async-start(bf16[8,16,448]{2,1,0:T(8,128)(2,1)} %bitcast.2), calls=%async_computation.1 | async-start | bytes 262144 | tf_op jit(solution)/shard_map/all_to_all | solution.py:28
  24.1 19.6 %all-to-all-start = ((bf16[8,2,28672]{2,1,0:T(2,128)(2,1)}), bf16[8,2,28672]{2,1,0:T(2,128)(2,1)S(1)}, u32[]{:S(2)}, u32[]{:S(2)}) async-start(bf16[8,2,28672]{2,1,0:T(2,128)(2,1)} %reshape.35), calls=%async_computation | async-start | bytes 1835008 | tf_op jit(solution)/shard_map/all_to_all | solution.py:36
  29.3 139.9 %all-gather.2.cloned.1.call-start = ((), (), s32[]{:S(2)}) async-start(), calls=%async_computation.3 | async-start | bytes 15597568 | tf_op jit(solution)/shard_map/all_gather | solution.py:41
  48.6 0.9 copy-start.2
Sparse Core Ops, SparseCore 0:
  67.7 101.4 all-gather.1
where the time goes:
time: 190 us; the launch traced here: 189 us
  waiting for transfers between devices  116 us (61%)
  local copies, waits for them, and re-layouts  23.2 us (12%)
  blocking collectives  17.1 us (9%)
  between operations  14.1 us (7%)
  starting transfers between devices  11.4 us (6%)
  other arithmetic  7.75 us (4%)
    all_gather x1, waiting for transfers between devices, shards(): weights = lax.all_gather(gathered, ('gx', 'gy'), axis=0, tiled=True)  102 us
    unnamed x11, local copies, waits for them, and re-layouts  22.3 us
    all_to_all x1, blocking collectives, from_everyone(): return lax.all_to_all(copies, axis, split_axis=0, concat_axis=0, tiled=True)  17.1 us
    all_to_all x1, waiting for transfers between devices, shards(): lax.all_to_all(compressed[:, None, :], 'gz', split_axis=0, concat_axis=1,...  14 us
    all_to_all x1, starting transfers between devices, shards(): lax.all_to_all(variance.astype(jnp.bfloat16), 'gz', split_axis=0, concat_...  6.19 us
    all_to_all x1, starting transfers between devices, shards(): lax.all_to_all(compressed[:, None, :], 'gz', split_axis=0, concat_axis=1,...  5.14 us
  transfers between devices with their start and end apart: 3, of which 2 were waited for; matrix products, arithmetic and copies ran while one was open for 5% of the time, Pallas kernels for 0%

commit v1 on v0

--- a/solution.py
+++ b/solution.py
@@ -38,7 +38,10 @@
     new_master = master - learning_rate * new_momentum / (jnp.sqrt(owned_variance) + epsilon)
     shard = new_master.astype(jnp.bfloat16)
     gathered = collect(shard, "gz", 0)
-    weights = lax.all_gather(gathered, ("gx", "gy"), axis=0, tiled=True)
+    n_dev = lax.axis_size(("gx", "gy"))
+    pieces = jnp.stack([gathered for _ in range(n_dev)])
+    pieces = lax.all_to_all(pieces, ("gx", "gy"), split_axis=0, concat_axis=0)
+    weights = jnp.concatenate(pieces, axis=0)
     return (weights, new_master, new_momentum, worker_error)
 
 

time: 190 us -> 246 us (1.29)
  blocking collectives: 17.1 us -> 188 us
  waiting for transfers between devices: 116 us -> 14.1 us
  between operations: 14.1 us -> 0.71 us
    all_to_all x0 -> x1, blocking collectives: none -> 172 us  [shards(): pieces = lax.all_to_all(pieces, ('gx', 'gy'), split_axis=0, concat_axis=0)]
    all_gather x1 -> x0, waiting for transfers between devices: 102 us -> none  [shards(): weights = lax.all_gather(gathered, ('gx', 'gy'), axis=0, tiled=True)]
    unnamed x11, local copies, waits for them, and re-layouts: 22.3 us -> 14.6 us
    another operation x0 -> x1, local copies, waits for them, and re-layouts: none -> 6.88 us  [shards(): pieces = jnp.stack([gathered for _ in range(n_dev)])]
  transfers between devices with their start and end apart: 3 -> 2, of which waited for: 2 -> 1; matrix products, arithmetic and copies ran while one was open for 5% -> 4% of each run, Pallas kernels for 0% -> 0%
where the time goes in v1:
time: 246 us; the launch traced here: 244 us
  blocking collectives  188 us (76%)
  local copies, waits for them, and re-layouts  22.4 us (9%)
  waiting for transfers between devices  14.1 us (6%)
  starting transfers between devices  11.3 us (5%)
  other arithmetic  7.75 us (3%)
    all_to_all x1, blocking collectives, shards(): pieces = lax.all_to_all(pieces, ('gx', 'gy'), split_axis=0, concat_axis=0)  172 us
    all_to_all x1, blocking collectives, from_everyone(): return lax.all_to_all(copies, axis, split_axis=0, concat_axis=0, tiled=True)  16.2 us
    unnamed x11, local copies, waits for them, and re-layouts  14.6 us
    all_to_all x1, waiting for transfers between devices, shards(): lax.all_to_all(compressed[:, None, :], 'gz', split_axis=0, concat_axis=1,...  14.1 us
    another operation x1, local copies, waits for them, and re-layouts, shards(): pieces = jnp.stack([gathered for _ in range(n_dev)])  6.88 us
    all_to_all x1, starting transfers between devices, shards(): lax.all_to_all(variance.astype(jnp.bfloat16), 'gz', split_axis=0, concat_...  6.19 us
    all_to_all x1, starting transfers between devices, shards(): lax.all_to_all(compressed[:, None, :], 'gz', split_axis=0, concat_axis=1,...  5.14 us
  transfers between devices with their start and end apart: 2, of which 1 were waited for; matrix products, arithmetic and copies ran while one was open for 4% of the time, Pallas kernels for 0%

profile of v1, /device:TPU:1, one launch (start us, length us, event | category | flops | bytes accessed | tf_op | source)
XLA Modules:
  0.0 244.0 jit_solution(1136089879532882368)
XLA Ops:
  0.6 0.0 copy-start
  0.6 0.0 copy-start.1
  0.7 1.8 copy.15
  2.5 6.2 %all-to-all-start.1 = ((bf16[8,16,448]{2,1,0:T(8,128)(2,1)}), bf16[8,16,448]{2,1,0:T(8,128)(2,1)S(1)}, u32[]{:S(2)}, u32[]{:S(2)}) async-start(bf16[8,16,448]{2,1,0:T(8,128)(2,1)} %bitcast.2), calls=%async_computation.1 | async-start | bytes 262144 | tf_op jit(solution)/shard_map/all_to_all | solution.py:28
  8.7 2.2 abs_reduce_fusion
  10.9 0.0 copy-done
  10.9 0.0 copy-done.1
  10.9 2.1 subtract_bitcast_fusion
  13.0 0.5 broadcast.15
  13.5 2.5 %reduce.3 = bf16[128,3584]{1,0:T(8,128)(2,1)S(1)} reduce(bf16[128,1,3584]{2,0,1:T(8,128)(2,1)} %get-tuple-element.7, bf16[]{:T(256)} %broadcast.15), dimensions={1}, to_apply=%copy.14.reduce_sub_computation | reduce | bytes 1835010 | tf_op jit(solution)/shard_map/broadcast_in_dim | solution.py:36
  16.0 1.6 reshape.37
  17.6 0.0 all-to-all-done.1
  17.6 5.1 %all-to-all-start = ((bf16[8,2,28672]{2,1,0:T(2,128)(2,1)}), bf16[8,2,28672]{2,1,0:T(2,128)(2,1)S(1)}, u32[]{:S(2)}, u32[]{:S(2)}) async-start(bf16[8,2,28672]{2,1,0:T(2,128)(2,1)} %reshape.37), calls=%async_computation | async-start | bytes 1835008 | tf_op jit(solution)/shard_map/all_to_all | solution.py:36
  22.7 0.1 add_bitcast_fusion
  22.8 0.2 copy.16
  23.0 0.1 add.19
  23.1 14.1 %all-to-all-done = bf16[8,2,28672]{2,1,0:T(2,128)(2,1)S(1)} async-done(((bf16[8,2,28672]{2,1,0:T(2,128)(2,1)}), bf16[8,2,28672]{2,1,0:T(2,128)(2,1)S(1)}, u32[]{:S(2)}, u32[]{:S(2)}) %all-to-all-start) | async-done | bytes 917536 | tf_op jit(solution)/shard_map/all_to_all | solution.py:36
  37.2 3.3 %reshape.38 = bf16[128,1,3584]{2,1,0:T(2,128)(2,1)} reshape(bf16[8,2,28672]{2,1,0:T(2,128)(2,1)S(1)} %all-to-all-done) | data formatting | bytes 1835008
  40.5 1.6 copy.17
  42.1 0.0 copy-start.2
  42.1 0.1 reduce_sum.19
  42.2 0.8 copy-done.2
  43.1 0.8 fusion.1
  43.9 0.1 broadcast_in_dim.21
  43.9 16.2 %all_to_all.32 = bf16[8,16,3584]{2,1,0:T(8,128)(2,1)S(1)} all-to-all(bf16[8,16,3584]{2,1,0:T(8,128)(2,1)S(1)} %broadcast_in_dim.21), channel_id=1, replica_groups=mesh['gx'=4,'gy'=4,'gz'=8] {'gz'}, dimensions={0} | all-to-all | bytes 1835008 | tf_op jit(solution)/shard_map/all_to_all | solution.py:13
  60.2 6.9 %stack.3 = bf16[16,128,3584]{2,1,0:T(8,128)(2,1)} broadcast(bf16[128,3584]{1,0:T(8,128)(2,1)S(1)} %bitcast.20), dimensions={1,2} | broadcast | bytes 15597568 | tf_op jit(solution)/shard_map/stack | solution.py:42
  67.0 171.5 %all_to_all.33 = bf16[16,128,3584]{2,1,0:T(8,128)(2,1)S(1)} all-to-all(bf16[16,128,3584]{2,1,0:T(8,128)(2,1)} %stack.3), channel_id=1, replica_groups=mesh['gx'=4,'gy'=4,'gz'=8] {'gx','gy'}, dimensions={0} | all-to-all | bytes 29360128 | tf_op jit(solution)/shard_map/all_to_all | solution.py:43
  238.6 5.5 %copy.20 = bf16[2048,3584]{1,0:T(8,128)(2,1)} copy(bf16[2048,3584]{1,0:T(8,128)(2,1)S(1)} %bitcast.18) | data formatting | bytes 29360128
  (1 shorter events, 0.0 us)
Async XLA Ops:
  0.6 10.3 %copy-start = (f32[128,3584]{1,0:T(8,128)S(1)}, f32[128,3584]{1,0:T(8,128)}, u32[]{:S(2)}) copy-start(f32[128,3584]{1,0:T(8,128)} %param.5) | copy-start | bytes 5505028
  0.6 10.3 %copy-start.1 = (bf16[1,128,3584]{2,1,0:T(8,128)(2,1)S(1)}, bf16[1,128,3584]{2,1,0:T(8,128)(2,1)}, u32[]{:S(2)}) copy-start(bf16[1,128,3584]{2,1,0:T(8,128)(2,1)} %param.4) | copy-start | bytes 2752516
  2.5 15.1 %all-to-all-start.1 = ((bf16[8,16,448]{2,1,0:T(8,128)(2,1)}), bf16[8,16,448]{2,1,0:T(8,128)(2,1)S(1)}, u32[]{:S(2)}, u32[]{:S(2)}) async-start(bf16[8,16,448]{2,1,0:T(8,128)(2,1)} %bitcast.2), calls=%async_computation.1 | async-start | bytes 262144 | tf_op jit(solution)/shard_map/all_to_all | solution.py:28
  17.6 19.6 %all-to-all-start = ((bf16[8,2,28672]{2,1,0:T(2,128)(2,1)}), bf16[8,2,28672]{2,1,0:T(2,128)(2,1)S(1)}, u32[]{:S(2)}, u32[]{:S(2)}) async-start(bf16[8,2,28672]{2,1,0:T(2,128)(2,1)} %reshape.37), calls=%async_computation | async-start | bytes 1835008 | tf_op jit(solution)/shard_map/all_to_all | solution.py:36
  42.1 0.9 copy-start.2
